TPU v7x, 32 devices: a whole 2x2x4 slice. The times are simulated.
32 devices in a mesh: prompt: 2 (over y), seq: 2 (over x), blk: 4 (over z), cfg: 2 (over core).
Axes of the slice: x: 2, y: 2, z: 4, core: 2. Of those that a mesh axis runs over, the one named last changes fastest.
Arguments:
- queries: bfloat16 [2, 384, 4096], P('cfg', ('prompt', 'blk', 'seq')), parts along dimension 1, may hold values from -5 to 5
- key_states: bfloat16 [2, 384, 4096], P('cfg', ('prompt', 'blk', 'seq')), parts along dimension 1, may hold values from -5 to 5
- value_states: bfloat16 [2, 384, 4096], P('cfg', ('prompt', 'blk', 'seq')), parts along dimension 1, may hold values from -6 to 6
- noisy_latents: float32 [384, 64], P(('prompt', 'blk', 'seq')), parts along dimension 0, may hold values from -6 to 6
- patch_order: int32 [384], P(('prompt', 'blk', 'seq')), parts along dimension 0, may hold values from 0 to 191, as said below
- head_weight: bfloat16 [4096, 64], replicated, may hold values from -0.75 to 0.75
- latent_std: float32 [16], replicated, may hold values from 0.1 to 1.9
- latent_mean: float32 [16], replicated, may hold values from -3 to 3
- conv_weight: bfloat16 [3, 3, 3, 16, 384], replicated, may hold values from -0.3125 to 0.3125
- conv_bias: float32 [384], replicated, may hold values from -2 to 2
Outputs:
- features: bfloat16 [8, 8, 24, 384], P(('prompt', 'cfg'), 'seq', 'blk'), parts along dimension 0
There are 2 independent parts, one for each index of `prompt`. A program takes and returns all parts, laid end to end along the dimension named above; an argument that names none is the same for every part. Nothing has to cross between parts.
Inputs may be any that keep to these rules, and one draw needn't show every extreme that they name: A permutation of 0 to 191 that keeps every aligned block of 24 tokens within itself: patch_order[t] // 24 == t // 24.
All inputs are finite; a program needn't handle non-finite values.
Results may differ from a plain program's by a relative error of at most 0.012.
Values may be sent and summed in bfloat16 or wider, within the bound.
No kernel may reach another device: no remote copies, remote signals or barrier semaphores. Data moves between devices by JAX's collectives and lax.ppermute only.
A program may use at most 128 MiB of HBM per device.

v0:
```python
import math

import jax
import jax.numpy as jnp
from jax import lax
from jax.sharding import PartitionSpec as P

HDIM = 128
ZCH = 16
COLS_DEV = 3


GUIDE = 5.0
NOISE_LEVEL = 0.5


def partner(array, axis, apart):
    return lax.ppermute(array, axis, [(i, i ^ 1 << apart) for i in range(lax.axis_size(axis))])


def padded(array, sides, width):
    for axis, dim in sides:
        devices, length = (lax.axis_size(axis), array.shape[dim])
        up = [(i, (i + 1) % devices) for i in range(devices - 1)]
        down = [(j, i) for i, j in up]
        last = lax.slice_in_dim(array, length - width, length, axis=dim)
        first = lax.slice_in_dim(array, 0, width, axis=dim)
        before = lax.ppermute(last, axis, up)
        after = lax.ppermute(first, axis, down)
        array = jnp.concatenate([before, array, after], axis=dim)
    return array


def fold_keys(carry, piece, grouped, block):
    keys_piece, values_piece = piece
    heads = grouped.shape[1]
    count = keys_piece.shape[0] // block
    key_blocks = keys_piece.reshape(count, block, heads, HDIM)
    value_blocks = values_piece.reshape(count, block, heads, HDIM)
    scale = 1.0 / math.sqrt(HDIM)

    def one_block(state, pair):
        top, total, acc = state
        key_block, value_block = pair
        scores = (
            jnp.einsum("qhd,khd->hqk", grouped, key_block, preferred_element_type=jnp.float32)
            * scale
        )
        new_top = jnp.maximum(top, jnp.max(scores, axis=2))
        expo = jnp.exp(scores - new_top[:, :, None])
        factor = jnp.exp(top - new_top)
        total = total * factor + jnp.sum(expo, axis=2)
        weights = expo.astype(jnp.bfloat16)
        update = jnp.einsum(
            "hqk,khd->qhd", weights, value_block, preferred_element_type=jnp.float32
        )
        acc = acc * factor.T[:, :, None] + update
        return ((new_top, total, acc), None)

    state, unused = lax.scan(one_block, carry, (key_blocks, value_blocks))
    return state


def start_for(rows, heads):
    return (
        jnp.full((heads, rows), -1e30, jnp.float32),
        jnp.zeros((heads, rows), jnp.float32),
        jnp.zeros((rows, heads, HDIM), jnp.float32),
    )


def finish(state):
    top, total, acc = state
    rows = acc.shape[0]
    return (acc / total.T[:, :, None]).astype(jnp.bfloat16).reshape(rows, acc.shape[1] * HDIM)


def local(
    queries,
    key_states,
    value_states,
    noisy_latents,
    patch_order,
    head_weight,
    latent_std,
    latent_mean,
    conv_weight,
    conv_bias,
):
    seq_count = lax.axis_size("seq")
    blk_count = lax.axis_size("blk")
    seq_index = lax.axis_index("seq")
    blk_index = lax.axis_index("blk")
    cfg_index = lax.axis_index("cfg")
    tok_rows = queries.shape[1]
    own_query = queries[0]
    own_keys = key_states[0]
    own_values = value_states[0]
    local_query, local_keys, local_values = (
        lax.all_to_all(own_query, "seq", split_axis=1, concat_axis=0, tiled=True),
        lax.all_to_all(own_keys, "seq", split_axis=1, concat_axis=0, tiled=True),
        lax.all_to_all(own_values, "seq", split_axis=1, concat_axis=0, tiled=True),
    )
    frame_rows = local_query.shape[0]
    half_feat = local_query.shape[1] // 2
    is_even = blk_index % 2 == 0

    def keep_give(whole):
        first = whole[:, :half_feat]
        second = whole[:, half_feat:]
        return (jnp.where(is_even, first, second), jnp.where(is_even, second, first))

    keep_q, give_q = keep_give(local_query)
    keep_k, give_k = keep_give(local_keys)
    keep_v, give_v = keep_give(local_values)
    got_q, got_k, got_v = partner((give_q, give_k, give_v), "blk", 0)

    def in_order(kept, got):
        return jnp.where(
            is_even, jnp.concatenate([kept, got], axis=0), jnp.concatenate([got, kept], axis=0)
        )

    pair_query = in_order(keep_q, got_q)
    held_keys = in_order(keep_k, got_k)
    held_values = in_order(keep_v, got_v)
    heads = half_feat // HDIM
    grouped = pair_query.reshape(2 * frame_rows, heads, HDIM)
    state = fold_keys(
        start_for(2 * frame_rows, heads), (held_keys, held_values), grouped, frame_rows
    )
    for bit in range(1, blk_count.bit_length() - 1):
        far_keys, far_values = partner((held_keys, held_values), "blk", bit)
        state = fold_keys(state, (far_keys, far_values), grouped, frame_rows)
        held_keys = jnp.concatenate([held_keys, far_keys], axis=0)
        held_values = jnp.concatenate([held_values, far_values], axis=0)
    paired_out = finish(state)
    mine_rows = jnp.where(is_even, paired_out[:frame_rows], paired_out[frame_rows:])
    their_rows = jnp.where(is_even, paired_out[frame_rows:], paired_out[:frame_rows])
    returned = partner(their_rows, "blk", 0)
    attended = jnp.where(
        is_even,
        jnp.concatenate([mine_rows, returned], axis=1),
        jnp.concatenate([returned, mine_rows], axis=1),
    )
    token_features = lax.all_to_all(attended, "seq", split_axis=0, concat_axis=1, tiled=True)
    velocity = jnp.dot(token_features, head_weight, preferred_element_type=jnp.float32)
    other = partner(velocity, "cfg", 0)
    is_cond = cfg_index == 0
    cond = jnp.where(is_cond, velocity, other)
    uncond = jnp.where(is_cond, other, velocity)
    guided = uncond + GUIDE * (cond - uncond)
    denoised = noisy_latents - NOISE_LEVEL * guided
    pixels = (
        denoised * jnp.tile(latent_std, 4)[None, :] + jnp.tile(latent_mean, 4)[None, :]
    ).astype(jnp.bfloat16)
    block_start = (blk_index * seq_count + seq_index) * tok_rows
    local_slot = patch_order - block_start
    selector = (jnp.arange(tok_rows, dtype=jnp.int32)[:, None] == local_slot[None, :]).astype(
        jnp.bfloat16
    )
    placed = jnp.dot(selector, pixels, preferred_element_type=jnp.float32).astype(jnp.bfloat16)
    grid_cols = COLS_DEV * blk_count
    strip_rows = tok_rows // grid_cols
    strip = placed.reshape(1, strip_rows, grid_cols * placed.shape[1])
    received = lax.all_to_all(strip, "blk", split_axis=2, concat_axis=0, tiled=True)
    frame_count = received.shape[0]
    tile = (
        received.reshape(frame_count, strip_rows, COLS_DEV, 2, 2, ZCH)
        .transpose(0, 1, 3, 2, 4, 5)
        .reshape(frame_count, 2 * strip_rows, 2 * COLS_DEV, ZCH)
    )
    half = frame_count // 2
    leading = jnp.zeros((2,) + tile.shape[1:], jnp.bfloat16)
    timeline = jnp.concatenate([leading, tile], axis=0)
    window = lax.dynamic_slice_in_dim(timeline, cfg_index * half, half + 2, 0)
    framed = padded(window, (("seq", 1), ("blk", 2)), 1)
    tile_rows = 2 * strip_rows
    tile_cols = 2 * COLS_DEV
    columns = []
    for step_t in range(3):
        for step_y in range(3):
            for step_x in range(3):
                columns.append(
                    framed[
                        step_t : step_t + half,
                        step_y : step_y + tile_rows,
                        step_x : step_x + tile_cols,
                        :,
                    ]
                )
    stacked = jnp.concatenate(columns, axis=3).reshape(half * tile_rows * tile_cols, 27 * ZCH)
    kernel = conv_weight.reshape(27 * ZCH, conv_weight.shape[4])
    output = jnp.dot(stacked, kernel, preferred_element_type=jnp.float32) + conv_bias[None, :]
    return output.reshape(half, tile_rows, tile_cols, conv_weight.shape[4]).astype(jnp.bfloat16)


def solution(mesh):
    in_specs = (
        P("cfg", ("prompt", "blk", "seq"), None),
        P("cfg", ("prompt", "blk", "seq"), None),
        P("cfg", ("prompt", "blk", "seq"), None),
        P(("prompt", "blk", "seq"), None),
        P(("prompt", "blk", "seq")),
        P(),
        P(),
        P(),
        P(),
        P(),
    )
    out_specs = P(("prompt", "cfg"), "seq", "blk", None)
    return jax.shard_map(local, mesh=mesh, in_specs=in_specs, out_specs=out_specs, check_vma=False)
```

profile of v0, /device:TPU:0, one launch (start us, length us, event | category | flops | bytes accessed | tf_op | source)
XLA Modules:
  0.0 94.7 jit_solution(8387433808589621011)
XLA Ops:
  1.9 4.4 %all-to-all-start.1 = ((bf16[24,2,2048]{2,0,1:T(8,128)(2,1)}), bf16[24,2,2048]{2,0,1:T(8,128)(2,1)S(1)}, u32[]{:S(2)}, u32[]{:S(2)}) async-start(bf16[24,2,2048]{2,0,1:T(8,128)(2,1)} %copy.55), calls=%async_computation.1 | async-start | bytes 393216 | tf_op jit(solution)/shard_map/all_to_all | solution.py:100
  8.2 3.2 %all-to-all-done.1 = bf16[24,2,2048]{2,0,1:T(8,128)(2,1)S(1)} async-done(((bf16[24,2,2048]{2,0,1:T(8,128)(2,1)}), bf16[24,2,2048]{2,0,1:T(8,128)(2,1)S(1)}, u32[]{:S(2)}, u32[]{:S(2)}) %all-to-all-start.1) | async-done | bytes 196640 | tf_op jit(solution)/shard_map/all_to_all | solution.py:100
  11.4 3.4 %all-to-all-start.2 = ((bf16[24,2,2048]{2,0,1:T(8,128)(2,1)}), bf16[24,2,2048]{2,0,1:T(8,128)(2,1)S(1)}, u32[]{:S(2)}, u32[]{:S(2)}) async-start(bf16[24,2,2048]{2,0,1:T(8,128)(2,1)} %copy.56), calls=%async_computation.2 | async-start | bytes 393216 | tf_op jit(solution)/shard_map/all_to_all | solution.py:102
  14.9 2.0 %collective-permute-start.1 = (bf16[48,1024]{1,0:T(8,128)(2,1)S(1)}, bf16[48,1024]{1,0:T(8,128)(2,1)S(1)}, u32[]{:S(2)}, u32[]{:S(2)}) collective-permute-start(bf16[48,1024]{1,0:T(8,128)(2,1)S(1)} %get-tuple-element.212), channel_id=1, source_target_pairs={{0,2},{2,0},{4,6},{6,4},{1,3},{3,1},{5,7},{7,5},{8,10},{10,8},{12,... | collective-permute-start | bytes 294920 | tf_op jit(solution)/shard_map/ppermute | solution.py:18
  16.8 2.8 %all-to-all-done.2 = bf16[24,2,2048]{2,0,1:T(8,128)(2,1)S(1)} async-done(((bf16[24,2,2048]{2,0,1:T(8,128)(2,1)}), bf16[24,2,2048]{2,0,1:T(8,128)(2,1)S(1)}, u32[]{:S(2)}, u32[]{:S(2)}) %all-to-all-start.2) | async-done | bytes 196640 | tf_op jit(solution)/shard_map/all_to_all | solution.py:102
  19.6 3.4 %all-to-all-start = ((bf16[24,2,2048]{2,0,1:T(8,128)(2,1)}), bf16[24,2,2048]{2,0,1:T(8,128)(2,1)S(1)}, u32[]{:S(2)}, u32[]{:S(2)}) async-start(bf16[24,2,2048]{2,0,1:T(8,128)(2,1)} %copy.54), calls=%async_computation | async-start | bytes 393216 | tf_op jit(solution)/shard_map/all_to_all | solution.py:101
  23.1 2.0 %collective-permute-start.2 = (bf16[48,1024]{1,0:T(8,128)(2,1)S(1)}, bf16[48,1024]{1,0:T(8,128)(2,1)S(1)}, u32[]{:S(2)}, u32[]{:S(2)}) collective-permute-start(bf16[48,1024]{1,0:T(8,128)(2,1)S(1)} %get-tuple-element.210), channel_id=1, source_target_pairs={{0,2},{2,0},{4,6},{6,4},{1,3},{3,1},{5,7},{7,5},{8,10},{10,8},{12,... | collective-permute-start | bytes 294920 | tf_op jit(solution)/shard_map/ppermute | solution.py:18
  25.1 2.8 %all-to-all-done = bf16[24,2,2048]{2,0,1:T(8,128)(2,1)S(1)} async-done(((bf16[24,2,2048]{2,0,1:T(8,128)(2,1)}), bf16[24,2,2048]{2,0,1:T(8,128)(2,1)S(1)}, u32[]{:S(2)}, u32[]{:S(2)}) %all-to-all-start) | async-done | bytes 196640 | tf_op jit(solution)/shard_map/all_to_all | solution.py:101
  27.9 2.0 %collective-permute-start = (bf16[48,1024]{1,0:T(8,128)(2,1)S(1)}, bf16[48,1024]{1,0:T(8,128)(2,1)S(1)}, u32[]{:S(2)}, u32[]{:S(2)}) collective-permute-start(bf16[48,1024]{1,0:T(8,128)(2,1)S(1)} %get-tuple-element.214), channel_id=1, source_target_pairs={{0,2},{2,0},{4,6},{6,4},{1,3},{3,1},{5,7},{7,5},{8,10},{10,8},{12,... | collective-permute-start | bytes 294920 | tf_op jit(solution)/shard_map/ppermute | solution.py:18
  30.0 2.7 %collective-permute-start.4 = (bf16[96,1024]{1,0:T(8,128)(2,1)S(1)}, bf16[96,1024]{1,0:T(8,128)(2,1)S(1)}, u32[]{:S(2)}, u32[]{:S(2)}) collective-permute-start(bf16[96,1024]{1,0:T(8,128)(2,1)S(1)} %maximum_select_fusion.2), channel_id=1, source_target_pairs={{0,4},{2,6},{4,0},{6,2},{1,5},{3,7},{5,1},{7,3},{8,12},{10,14},{12... | collective-permute-start | bytes 589832 | tf_op jit(solution)/shard_map/ppermute | solution.py:18
  32.8 3.0 %collective-permute-start.3 = (bf16[96,1024]{1,0:T(8,128)(2,1)S(1)}, bf16[96,1024]{1,0:T(8,128)(2,1)S(1)}, u32[]{:S(2)}, u32[]{:S(2)}) collective-permute-start(bf16[96,1024]{1,0:T(8,128)(2,1)S(1)} %maximum_select_fusion), channel_id=1, source_target_pairs={{0,4},{2,6},{4,0},{6,2},{1,5},{3,7},{5,1},{7,3},{8,12},{10,14},{12... | collective-permute-start | bytes 589832 | tf_op jit(solution)/shard_map/ppermute | solution.py:18
  35.9 1.5 %while.30 = (s32[]{:T(128)}, f32[8,96]{1,0:T(8,128)S(1)}, f32[8,96]{1,0:T(8,128)S(1)}, f32[96,8,128]{2,0,1:T(8,128)S(1)}, bf16[2,48,8,128]{3,2,1,0:T(8,128)(2,1)...) while((s32[]{:T(128)}, f32[8,96]{1,0:T(8,128)S(1)}, ...), condition=%wide.region_3.4_spmd.clone, body=%wide.region_0.3_spmd.clone.sunk | while | flops 19395076 | bytes 2064493 | solution.py:60
  37.3 7.1 %collective-permute-done.4 = bf16[96,1024]{1,0:T(8,128)(2,1)S(1)} collective-permute-done((bf16[96,1024]{1,0:T(8,128)(2,1)S(1)}, bf16[96,1024]{1,0:T(8,128)(2,1)S(1)}, u32[]{:S(2)}, u32[]{:S(2)}) %collective-permute-start.4) | collective-permute-done | bytes 196640 | tf_op jit(solution)/shard_map/ppermute | solution.py:18
  44.5 2.1 %collective-permute-done.3 = bf16[96,1024]{1,0:T(8,128)(2,1)S(1)} collective-permute-done((bf16[96,1024]{1,0:T(8,128)(2,1)S(1)}, bf16[96,1024]{1,0:T(8,128)(2,1)S(1)}, u32[]{:S(2)}, u32[]{:S(2)}) %collective-permute-start.3) | collective-permute-done | bytes 196640 | tf_op jit(solution)/shard_map/ppermute | solution.py:18
  46.6 1.5 %while.29 = (s32[]{:T(128)}, f32[8,96]{1,0:T(8,128)S(1)}, f32[8,96]{1,0:T(8,128)S(1)}, f32[96,8,128]{2,0,1:T(8,128)S(1)}, bf16[2,48,8,128]{3,2,1,0:T(8,128)(2,1)...) while((s32[]{:T(128)}, f32[8,96]{1,0:T(8,128)S(1)}, ...), condition=%wide.region_7.8_spmd, body=%wide.region_4.7_spmd.sunk | while | flops 19294464 | bytes 2064473 | solution.py:60
  48.5 4.5 %collective-permute-done.5 = bf16[48,1024]{1,0:T(8,128)(2,1)S(1)} collective-permute-done((bf16[48,1024]{1,0:T(8,128)(2,1)S(1)}, bf16[48,1024]{1,0:T(8,128)(2,1)S(1)}, u32[]{:S(2)}, u32[]{:S(2)}) %collective-permute-start.5) | collective-permute-done | bytes 98336 | tf_op jit(solution)/shard_map/ppermute | solution.py:18
  53.7 3.4 %all-to-all-start.3 = ((bf16[2,24,2048]{2,1,0:T(8,128)(2,1)}), bf16[2,24,2048]{2,1,0:T(8,128)(2,1)S(1)}, u32[]{:S(2)}, u32[]{:S(2)}) async-start(bf16[2,24,2048]{2,1,0:T(8,128)(2,1)} %maximum_select_fusion.3), calls=%async_computation.3 | async-start | bytes 393216 | tf_op jit(solution)/shard_map/all_to_all | solution.py:145
  57.2 4.8 %all-to-all-done.3 = bf16[2,24,2048]{2,1,0:T(8,128)(2,1)S(1)} async-done(((bf16[2,24,2048]{2,1,0:T(8,128)(2,1)}), bf16[2,24,2048]{2,1,0:T(8,128)(2,1)S(1)}, u32[]{:S(2)}, u32[]{:S(2)}) %all-to-all-start.3) | async-done | bytes 196640 | tf_op jit(solution)/shard_map/all_to_all | solution.py:145
  64.6 1.9 %reduce = bf16[768,2]{1,0:T(8,128)(2,1)S(1)} reduce(bf16[768,1,2]{2,1,0:T(2,128)(2,1)S(1)} %bitcast.107, bf16[]{:T(256)} %broadcast.67), dimensions={1}, to_apply=%bitcast.69.reduce_sub_computation | reduce | bytes 6146
  67.3 4.0 %all-to-all-start.4 = ((bf16[4,2,192]{2,1,0:T(2,128)(2,1)}), bf16[4,2,192]{2,1,0:T(2,128)(2,1)S(1)}, u32[]{:S(2)}, u32[]{:S(2)}) async-start(bf16[4,2,192]{2,1,0:T(2,128)(2,1)} %reshape.85), calls=%async_computation.4 | async-start | bytes 8192 | tf_op jit(solution)/shard_map/all_to_all | solution.py:165
  71.3 5.6 %all-to-all-done.4 = bf16[4,2,192]{2,1,0:T(2,128)(2,1)S(1)} async-done(((bf16[4,2,192]{2,1,0:T(2,128)(2,1)}), bf16[4,2,192]{2,1,0:T(2,128)(2,1)S(1)}, u32[]{:S(2)}, u32[]{:S(2)}) %all-to-all-start.4) | async-done | bytes 3104 | tf_op jit(solution)/shard_map/all_to_all | solution.py:165
  77.9 1.9 %collective-permute-start.7 = (bf16[4,1,6,16]{3,1,2,0:T(2,128)(2,1)S(1)}, bf16[4,1,6,16]{3,1,2,0:T(2,128)(2,1)S(1)}, u32[]{:S(2)}, u32[]{:S(2)}) collective-permute-start(bf16[4,1,6,16]{3,1,2,0:T(2,128)(2,1)S(1)} %get-tuple-element.249), channel_id=1, source_target_pairs={{0,8},{1,9},{2,10},{3,11},{4,12},{5,13},{6,14},{7,15},{16,24},{17,... | collective-permute-start | bytes 2312 | tf_op jit(solution)/shard_map/ppermute | solution.py:28
  81.2 4.2 %collective-permute-done.8 = bf16[4,1,6,16]{3,1,2,0:T(2,128)(2,1)S(1)} collective-permute-done((bf16[4,1,6,16]{3,1,2,0:T(2,128)(2,1)S(1)}, bf16[4,1,6,16]{3,1,2,0:T(2,128)(2,1)S(1)}, u32[]{:S(2)}, u32[]{:S(2)}) %collective-permute-start.8) | collective-permute-done | bytes 800 | tf_op jit(solution)/shard_map/ppermute | solution.py:29
  86.8 4.5 %collective-permute-start.9 = (bf16[4,6,1,16]{3,1,2,0:T(8,128)(2,1)S(1)}, bf16[4,6,1,16]{3,1,2,0:T(8,128)(2,1)S(1)}, u32[]{:S(2)}, u32[]{:S(2)}) collective-permute-start(bf16[4,6,1,16]{3,1,2,0:T(8,128)(2,1)S(1)} %get-tuple-element.236), channel_id=1, source_target_pairs={{0,2},{2,4},{4,6},{1,3},{3,5},{5,7},{8,10},{10,12},{12,14},{9,11},... | collective-permute-start | bytes 2312 | tf_op jit(solution)/shard_map/ppermute | solution.py:28
  (116 shorter events, 18.3 us)
Async XLA Ops:
  0.0 62.0 %copy-start = (bf16[4096,64]{0,1:T(8,128)(2,1)S(1)}, bf16[4096,64]{0,1:T(8,128)(2,1)}, u32[]{:S(2)}) copy-start(bf16[4096,64]{0,1:T(8,128)(2,1)} %param.19) | copy-start | bytes 1572868
  1.9 4.4 %copy-start.2 = (bf16[1,24,4096]{2,1,0:T(8,128)(2,1)S(1)}, bf16[1,24,4096]{2,1,0:T(8,128)(2,1)}, u32[]{:S(2)}) copy-start(bf16[1,24,4096]{2,1,0:T(8,128)(2,1)} %param.16) | copy-start | bytes 589828
  1.9 9.5 %all-to-all-start.1 = ((bf16[24,2,2048]{2,0,1:T(8,128)(2,1)}), bf16[24,2,2048]{2,0,1:T(8,128)(2,1)S(1)}, u32[]{:S(2)}, u32[]{:S(2)}) async-start(bf16[24,2,2048]{2,0,1:T(8,128)(2,1)} %copy.55), calls=%async_computation.1 | async-start | bytes 393216 | tf_op jit(solution)/shard_map/all_to_all | solution.py:100
  6.4 0.9 copy-start.3
  11.4 8.2 %all-to-all-start.2 = ((bf16[24,2,2048]{2,0,1:T(8,128)(2,1)}), bf16[24,2,2048]{2,0,1:T(8,128)(2,1)S(1)}, u32[]{:S(2)}, u32[]{:S(2)}) async-start(bf16[24,2,2048]{2,0,1:T(8,128)(2,1)} %copy.56), calls=%async_computation.2 | async-start | bytes 393216 | tf_op jit(solution)/shard_map/all_to_all | solution.py:102
  14.9 15.0 %collective-permute-start.1 = (bf16[48,1024]{1,0:T(8,128)(2,1)S(1)}, bf16[48,1024]{1,0:T(8,128)(2,1)S(1)}, u32[]{:S(2)}, u32[]{:S(2)}) collective-permute-start(bf16[48,1024]{1,0:T(8,128)(2,1)S(1)} %get-tuple-element.212), channel_id=1, source_target_pairs={{0,2},{2,0},{4,6},{6,4},{1,3},{3,1},{5,7},{7,5},{8,10},{10,8},{12,... | collective-permute-start | bytes 294920 | tf_op jit(solution)/shard_map/ppermute | solution.py:18
  19.6 8.2 %all-to-all-start = ((bf16[24,2,2048]{2,0,1:T(8,128)(2,1)}), bf16[24,2,2048]{2,0,1:T(8,128)(2,1)S(1)}, u32[]{:S(2)}, u32[]{:S(2)}) async-start(bf16[24,2,2048]{2,0,1:T(8,128)(2,1)} %copy.54), calls=%async_computation | async-start | bytes 393216 | tf_op jit(solution)/shard_map/all_to_all | solution.py:101
  23.1 6.8 %collective-permute-start.2 = (bf16[48,1024]{1,0:T(8,128)(2,1)S(1)}, bf16[48,1024]{1,0:T(8,128)(2,1)S(1)}, u32[]{:S(2)}, u32[]{:S(2)}) collective-permute-start(bf16[48,1024]{1,0:T(8,128)(2,1)S(1)} %get-tuple-element.210), channel_id=1, source_target_pairs={{0,2},{2,0},{4,6},{6,4},{1,3},{3,1},{5,7},{7,5},{8,10},{10,8},{12,... | collective-permute-start | bytes 294920 | tf_op jit(solution)/shard_map/ppermute | solution.py:18
  27.9 4.8 %collective-permute-start = (bf16[48,1024]{1,0:T(8,128)(2,1)S(1)}, bf16[48,1024]{1,0:T(8,128)(2,1)S(1)}, u32[]{:S(2)}, u32[]{:S(2)}) collective-permute-start(bf16[48,1024]{1,0:T(8,128)(2,1)S(1)} %get-tuple-element.214), channel_id=1, source_target_pairs={{0,2},{2,0},{4,6},{6,4},{1,3},{3,1},{5,7},{7,5},{8,10},{10,8},{12,... | collective-permute-start | bytes 294920 | tf_op jit(solution)/shard_map/ppermute | solution.py:18
  30.0 14.4 %collective-permute-start.4 = (bf16[96,1024]{1,0:T(8,128)(2,1)S(1)}, bf16[96,1024]{1,0:T(8,128)(2,1)S(1)}, u32[]{:S(2)}, u32[]{:S(2)}) collective-permute-start(bf16[96,1024]{1,0:T(8,128)(2,1)S(1)} %maximum_select_fusion.2), channel_id=1, source_target_pairs={{0,4},{2,6},{4,0},{6,2},{1,5},{3,7},{5,1},{7,3},{8,12},{10,14},{12... | collective-permute-start | bytes 589832 | tf_op jit(solution)/shard_map/ppermute | solution.py:18
  32.8 13.8 %collective-permute-start.3 = (bf16[96,1024]{1,0:T(8,128)(2,1)S(1)}, bf16[96,1024]{1,0:T(8,128)(2,1)S(1)}, u32[]{:S(2)}, u32[]{:S(2)}) collective-permute-start(bf16[96,1024]{1,0:T(8,128)(2,1)S(1)} %maximum_select_fusion), channel_id=1, source_target_pairs={{0,4},{2,6},{4,0},{6,2},{1,5},{3,7},{5,1},{7,3},{8,12},{10,14},{12... | collective-permute-start | bytes 589832 | tf_op jit(solution)/shard_map/ppermute | solution.py:18
  48.3 4.7 %collective-permute-start.5 = (bf16[48,1024]{1,0:T(8,128)(2,1)S(1)}, bf16[48,1024]{1,0:T(8,128)(2,1)S(1)}, u32[]{:S(2)}, u32[]{:S(2)}) collective-permute-start(bf16[48,1024]{1,0:T(8,128)(2,1)S(1)} %bitcast.125), channel_id=1, source_target_pairs={{0,2},{2,0},{4,6},{6,4},{1,3},{3,1},{5,7},{7,5},{8,10},{10,8},{12,... | collective-permute-start | bytes 294920 | tf_op jit(solution)/shard_map/ppermute | solution.py:18
  53.7 8.2 %all-to-all-start.3 = ((bf16[2,24,2048]{2,1,0:T(8,128)(2,1)}), bf16[2,24,2048]{2,1,0:T(8,128)(2,1)S(1)}, u32[]{:S(2)}, u32[]{:S(2)}) async-start(bf16[2,24,2048]{2,1,0:T(8,128)(2,1)} %maximum_select_fusion.3), calls=%async_computation.3 | async-start | bytes 393216 | tf_op jit(solution)/shard_map/all_to_all | solution.py:145
  62.0 0.7 copy-start.8
  62.0 0.7 copy-start.6
  62.3 1.2 %copy-start.4 = (f32[24,64]{1,0:T(8,128)S(1)}, f32[24,64]{1,0:T(8,128)}, u32[]{:S(2)}) copy-start(f32[24,64]{1,0:T(8,128)} %param.17) | copy-start | bytes 18436
  62.3 1.2 %collective-permute-start.6 = (f32[24,64]{1,0:T(8,128)S(1)}, f32[24,64]{1,0:T(8,128)S(1)}, u32[]{:S(2)}, u32[]{:S(2)}) collective-permute-start(f32[24,64]{1,0:T(8,128)S(1)} %fusion.28), channel_id=1, source_target_pairs={{0,1},{1,0},{2,3},{3,2},{4,5},{5,4},{6,7},{7,6},{8,9},{9,8},{10,11... | collective-permute-start | bytes 18440 | tf_op jit(solution)/shard_map/ppermute | solution.py:18
  67.3 9.5 %all-to-all-start.4 = ((bf16[4,2,192]{2,1,0:T(2,128)(2,1)}), bf16[4,2,192]{2,1,0:T(2,128)(2,1)S(1)}, u32[]{:S(2)}, u32[]{:S(2)}) async-start(bf16[4,2,192]{2,1,0:T(2,128)(2,1)} %reshape.85), calls=%async_computation.4 | async-start | bytes 8192 | tf_op jit(solution)/shard_map/all_to_all | solution.py:165
  77.9 3.3 %collective-permute-start.7 = (bf16[4,1,6,16]{3,1,2,0:T(2,128)(2,1)S(1)}, bf16[4,1,6,16]{3,1,2,0:T(2,128)(2,1)S(1)}, u32[]{:S(2)}, u32[]{:S(2)}) collective-permute-start(bf16[4,1,6,16]{3,1,2,0:T(2,128)(2,1)S(1)} %get-tuple-element.249), channel_id=1, source_target_pairs={{0,8},{1,9},{2,10},{3,11},{4,12},{5,13},{6,14},{7,15},{16,24},{17,... | collective-permute-start | bytes 2312 | tf_op jit(solution)/shard_map/ppermute | solution.py:28
  79.8 5.6 %collective-permute-start.8 = (bf16[4,1,6,16]{3,1,2,0:T(2,128)(2,1)S(1)}, bf16[4,1,6,16]{3,1,2,0:T(2,128)(2,1)S(1)}, u32[]{:S(2)}, u32[]{:S(2)}) collective-permute-start(bf16[4,1,6,16]{3,1,2,0:T(2,128)(2,1)S(1)} %get-tuple-element.250), channel_id=1, source_target_pairs={{8,0},{9,1},{10,2},{11,3},{12,4},{13,5},{14,6},{15,7},{24,16},{25,... | collective-permute-start | bytes 2312 | tf_op jit(solution)/shard_map/ppermute | solution.py:29
  85.5 6.0 %collective-permute-start.10 = (bf16[4,6,1,16]{3,1,2,0:T(8,128)(2,1)S(1)}, bf16[4,6,1,16]{3,1,2,0:T(8,128)(2,1)S(1)}, u32[]{:S(2)}, u32[]{:S(2)}) collective-permute-start(bf16[4,6,1,16]{3,1,2,0:T(8,128)(2,1)S(1)} %get-tuple-element.235), channel_id=1, source_target_pairs={{2,0},{4,2},{6,4},{3,1},{5,3},{7,5},{10,8},{12,10},{14,12},{11,9},... | collective-permute-start | bytes 2312 | tf_op jit(solution)/shard_map/ppermute | solution.py:29
  86.8 5.9 %collective-permute-start.9 = (bf16[4,6,1,16]{3,1,2,0:T(8,128)(2,1)S(1)}, bf16[4,6,1,16]{3,1,2,0:T(8,128)(2,1)S(1)}, u32[]{:S(2)}, u32[]{:S(2)}) collective-permute-start(bf16[4,6,1,16]{3,1,2,0:T(8,128)(2,1)S(1)} %get-tuple-element.236), channel_id=1, source_target_pairs={{0,2},{2,4},{4,6},{1,3},{3,5},{5,7},{8,10},{10,12},{12,14},{9,11},... | collective-permute-start | bytes 2312 | tf_op jit(solution)/shard_map/ppermute | solution.py:28
  92.8 1.0 %copy-start.1 = (bf16[3,3,3,16,384]{4,3,2,1,0:T(8,128)(2,1)S(1)}, bf16[3,3,3,16,384]{4,3,2,1,0:T(8,128)(2,1)}, u32[]{:S(2)}) copy-start(bf16[3,3,3,16,384]{4,3,2,1,0:T(8,128)(2,1)} %param.22) | copy-start | bytes 995332
  92.9 1.0 %copy-start.5 = (f32[384]{0:T(512)S(1)}, f32[384]{0:T(512)}, u32[]{:S(2)}) copy-start(f32[384]{0:T(512)} %param.23) | copy-start | bytes 4612
  (1 other events, 0.7 us)
where the time goes:
time: 95.3 us; the launch traced here: 94.7 us
  starting transfers between devices  39.4 us (41%)
  waiting for transfers between devices  38.4 us (40%)
  local copies, waits for them, and re-layouts  9.88 us (10%)
  other arithmetic  3.41 us (4%)
  matrix products  2.88 us (3%)
    ppermute x7, waiting for transfers between devices, partner(): lax.ppermute(array, axis, [(i, i ^ 1 << apart) for i in range(lax.axis_si...  13.8 us
    ppermute x7, starting transfers between devices, partner(): lax.ppermute(array, axis, [(i, i ^ 1 << apart) for i in range(lax.axis_si...  11.7 us
    ppermute x2, starting transfers between devices, padded(): before = lax.ppermute(last, axis, up)  6.46 us
    all_to_all x1, waiting for transfers between devices, local(): lax.all_to_all(strip, 'blk', split_axis=2, concat_axis=0, tiled=True)  5.58 us
    all_to_all x1, waiting for transfers between devices, local(): lax.all_to_all(attended, 'seq', split_axis=0, concat_axis=1, tiled=True)  4.8 us
    all_to_all x1, starting transfers between devices, local(): lax.all_to_all(own_query, 'seq', split_axis=1, concat_axis=0, tiled=True)  4.37 us
    ppermute x2, waiting for transfers between devices, padded(): after = lax.ppermute(first, axis, down)  4.19 us
    all_to_all x1, starting transfers between devices, local(): lax.all_to_all(strip, 'blk', split_axis=2, concat_axis=0, tiled=True)  3.96 us
  transfers between devices with their start and end apart: 16, of which 11 were waited for; matrix products, arithmetic and copies ran while one was open for 4% of the time, Pallas kernels for 0%

commit v1 on v0

--- a/solution.py
+++ b/solution.py
@@ -2,7 +2,10 @@
 
 import jax
 import jax.numpy as jnp
+import numpy as np
 from jax import lax
+from jax.experimental import pallas as pl
+from jax.experimental.pallas import tpu as pltpu
 from jax.sharding import PartitionSpec as P
 
 HDIM = 128
@@ -194,6 +197,284 @@
     return output.reshape(half, tile_rows, tile_cols, conv_weight.shape[4]).astype(jnp.bfloat16)
 
 
+def pack_kernel(order_ref, start_ref, q_ref, k_ref, v_ref, noisy_ref, send_ref, noise_ref):
+    groups, rows, width = send_ref.shape
+    feat = width // 3
+    slot = order_ref[...] - start_ref[0]
+    hit = lax.broadcasted_iota(jnp.int32, (rows, rows), 0) == slot
+    selector = hit.astype(jnp.bfloat16)
+    ordered = jnp.dot(selector, q_ref[...], preferred_element_type=jnp.float32)
+    ordered = ordered.astype(jnp.bfloat16)
+    for group in range(groups):
+        cols = slice(group * feat, (group + 1) * feat)
+        send_ref[group, :, :feat] = ordered[:, cols]
+        send_ref[group, :, feat : 2 * feat] = k_ref[:, cols]
+        send_ref[group, :, 2 * feat :] = v_ref[:, cols]
+    noise_ref[...] = jnp.dot(
+        hit.astype(jnp.float32),
+        noisy_ref[...],
+        preferred_element_type=jnp.float32,
+        precision=lax.Precision.HIGHEST,
+    )
+
+
+def attend_kernel(place_ref, qkv_ref, weight_ref, noise_ref, pick_ref, out_ref, acc_ref):
+    tokens, width = qkv_ref.shape
+    feat = width // 3
+    block = noise_ref.shape[0]
+    scale = 1.0 / math.sqrt(HDIM)
+    total_velocity = jnp.zeros(acc_ref.shape, jnp.float32)
+    for head in range(feat // HDIM):
+        low = head * HDIM
+        query = qkv_ref[:, low : low + HDIM]
+        key = qkv_ref[:, feat + low : feat + low + HDIM]
+        value = qkv_ref[:, 2 * feat + low : 2 * feat + low + HDIM]
+        scores = (
+            lax.dot_general(
+                query, key, (((1,), (1,)), ((), ())), preferred_element_type=jnp.float32
+            )
+            * scale
+        )
+        expo = jnp.exp(scores - jnp.max(scores, axis=1, keepdims=True))
+        total = jnp.sum(expo, axis=1, keepdims=True)
+        mixed = jnp.dot(
+            expo.astype(jnp.bfloat16), value, preferred_element_type=jnp.float32
+        )
+        mixed = (mixed / total).astype(jnp.bfloat16)
+        total_velocity = total_velocity + jnp.dot(
+            mixed, weight_ref[low : low + HDIM, :], preferred_element_type=jnp.float32
+        )
+    is_cond = place_ref[1] == 0
+    factor = jnp.where(is_cond, -NOISE_LEVEL * GUIDE, -NOISE_LEVEL * (1.0 - GUIDE))
+    acc_ref[...] = total_velocity * factor
+    rows = pl.ds(pl.multiple_of(place_ref[0] * block, 8), block)
+    acc_ref[rows, :] = acc_ref[rows, :] + noise_ref[...] * jnp.where(is_cond, 1.0, 0.0)
+    share = acc_ref[...].astype(jnp.bfloat16)
+    both = jnp.concatenate([share[: tokens // 2], share[tokens // 2 :]], axis=1)
+    placed = jnp.dot(pick_ref[...], both, preferred_element_type=jnp.float32)
+    placed = placed.astype(jnp.bfloat16)
+    rows_each = out_ref.shape[2]
+    for group in range(out_ref.shape[0]):
+        piece = placed[group * rows_each : (group + 1) * rows_each]
+        for core in range(out_ref.shape[1]):
+            out_ref[group, core] = piece
+
+
+def conv_kernel(
+    place_ref, got_ref, std_ref, mean_ref, mesh_ref, weight_ref, bias_ref, order_ref, out_ref, big_ref
+):
+    frames_out, tile_rows, tile_cols, channels = out_ref.shape
+    wide = tile_cols // 2
+    high = tile_rows // 2
+    shares, rows, lanes = got_ref.shape
+    summed = got_ref[0].astype(jnp.float32)
+    for share in range(1, shares):
+        summed = summed + got_ref[share].astype(jnp.float32)
+    span = wide + 2
+    tall = high + 2
+    row = lax.broadcasted_iota(jnp.int32, (rows, lanes), 0)
+    col_at = place_ref[0] * wide - 1 + row % span
+    row_at = place_ref[1] * high - 1 + row // span % tall
+    inside = (
+        (col_at >= 0) & (col_at < place_ref[3]) & (row_at >= 0) & (row_at < place_ref[4])
+    )
+    pixels = jnp.where(inside, summed * std_ref[...] + mean_ref[...], 0.0)
+    half = lanes // 2
+    flat = jnp.concatenate([pixels[:, :half], pixels[:, half:]], axis=0)
+    count = 2 * rows
+    moved = pltpu.roll(flat, count - 1, 0)
+    pairs = jnp.concatenate([flat, moved], axis=1).astype(jnp.bfloat16)
+    wanted = mesh_ref[:, 0:1] + place_ref[2] * (frames_out * tall * span)
+    hits = (lax.broadcasted_iota(jnp.int32, (mesh_ref.shape[0], count), 1) == wanted).astype(
+        jnp.bfloat16
+    )
+    pieces = jnp.dot(hits, pairs, preferred_element_type=jnp.float32).astype(jnp.bfloat16)
+    part = frames_out * high * wide
+    part = (part + 15) // 16 * 16
+    big_ref[...] = jnp.zeros(big_ref.shape, big_ref.dtype)
+    results = []
+    for down in range(2):
+        for right in range(2):
+            which = down * 2 + right
+            for step_t in range(3):
+                for step_y in range(3):
+                    for step_x in range(3):
+                        y = 1 - down + step_y
+                        x = 1 - right + step_x
+                        at = (step_t * 2 + y // 2) * 8 + (x // 2) * 4 + (y % 2) * 2 + x % 2
+                        big_ref[which, at * ZCH : (at + 1) * ZCH, :] = weight_ref[
+                            (step_t * 3 + step_y) * 3 + step_x
+                        ]
+            columns = []
+            for step_t in range(3):
+                for near in range(2):
+                    at = (step_t * 3 + down + near) * 2 + right
+                    columns.append(pieces[at * part : (at + 1) * part])
+            stacked = jnp.concatenate(columns, axis=1)
+            result = jnp.dot(stacked, big_ref[which], preferred_element_type=jnp.float32)
+            results.append((result + bias_ref[...]).astype(jnp.bfloat16))
+    together = jnp.concatenate(results, axis=0)
+    final = jnp.dot(order_ref[...], together, preferred_element_type=jnp.float32)
+    final = final.astype(jnp.bfloat16)
+    for frame in range(frames_out):
+        for y in range(tile_rows):
+            at = (frame * tile_rows + y) * 8
+            out_ref[frame, y] = final[at : at + tile_cols]
+
+
+def tile_rows_of(seq_count, blk_count, frames, high, wide):
+    grid_rows = seq_count * high
+    grid_cols = blk_count * wide
+    table = np.full((blk_count, seq_count, frames // 2, high + 2, wide + 2), -1, np.int32)
+    for blk in range(blk_count):
+        for seq in range(seq_count):
+            for frame in range(frames // 2):
+                for i in range(high + 2):
+                    for w in range(wide + 2):
+                        y = seq * high - 1 + i
+                        x = blk * wide - 1 + w
+                        if 0 <= y < grid_rows and 0 <= x < grid_cols:
+                            table[blk, seq, frame, i, w] = (frame * grid_rows + y) * grid_cols + x
+    return table.reshape(-1)
+
+
+def window_rows(frames_out, high, wide):
+    part = (frames_out * high * wide + 15) // 16 * 16
+    table = np.full((3, 3, 2, part), -100000, np.int32)
+    for step_t in range(3):
+        for near in range(3):
+            for right in range(2):
+                for frame in range(frames_out):
+                    for i in range(high):
+                        for w in range(wide):
+                            source = frame - 2 + step_t
+                            at = (source * (high + 2) + i + near) * (wide + 2) + w + right
+                            if source < 0:
+                                at = (source * (high + 2) + i + near) * (wide + 2) + w + right
+                            table[step_t, near, right, (frame * high + i) * wide + w] = at
+    return table.reshape(-1, 1)
+
+
+def output_order(frames_out, high, wide):
+    part = (frames_out * high * wide + 15) // 16 * 16
+    table = np.zeros((frames_out * 2 * high * 8, 4 * part), np.float32)
+    for frame in range(frames_out):
+        for y in range(2 * high):
+            for x in range(2 * wide):
+                which = (y % 2) * 2 + x % 2
+                source = which * part + (frame * high + y // 2) * wide + x // 2
+                table[(frame * 2 * high + y) * 8 + x, source] = 1.0
+    return table
+
+
+def exchange(packed):
+    return lax.all_to_all(packed, ("blk", "seq"), split_axis=0, concat_axis=0, tiled=True)
+
+
+def by_heads(
+    queries,
+    key_states,
+    value_states,
+    noisy_latents,
+    patch_order,
+    head_weight,
+    latent_std,
+    latent_mean,
+    conv_weight,
+    conv_bias,
+):
+    seq_count = lax.axis_size("seq")
+    blk_count = lax.axis_size("blk")
+    cfg_count = lax.axis_size("cfg")
+    seq_index = lax.axis_index("seq")
+    blk_index = lax.axis_index("blk")
+    cfg_index = lax.axis_index("cfg")
+    groups = seq_count * blk_count
+    block = queries.shape[1]
+    tokens = groups * block
+    feat = queries.shape[2] // groups
+    patch = noisy_latents.shape[1]
+    channels = conv_weight.shape[4]
+    own = (blk_index * seq_count + seq_index).astype(jnp.int32)
+    frames = blk_count
+    grid_cols = COLS_DEV * blk_count
+    high = block // grid_cols
+    wide = COLS_DEV
+    vmem = pl.BlockSpec(memory_space=pltpu.VMEM)
+    smem = pl.BlockSpec(memory_space=pltpu.SMEM)
+    packed, noise = pl.pallas_call(
+        pack_kernel,
+        out_shape=(
+            jax.ShapeDtypeStruct((groups, block, 3 * feat), jnp.bfloat16),
+            jax.ShapeDtypeStruct((block, patch), jnp.float32),
+        ),
+        in_specs=[vmem, smem, vmem, vmem, vmem, vmem],
+        out_specs=(vmem, vmem),
+    )(
+        patch_order[None, :],
+        (own * block)[None],
+        queries[0],
+        key_states[0],
+        value_states[0],
+        noisy_latents,
+    )
+    received = exchange(packed).reshape(tokens, 3 * feat)
+    weight = lax.dynamic_slice_in_dim(head_weight, own * feat, feat, 0)
+    pick = (
+        np.arange(tokens // 2)[None, :]
+        == tile_rows_of(seq_count, blk_count, frames, high, wide)[:, None]
+    )
+    tile = frames // 2 * (high + 2) * (wide + 2)
+    shares = pl.pallas_call(
+        attend_kernel,
+        out_shape=jax.ShapeDtypeStruct((groups, cfg_count, tile, 2 * patch), jnp.bfloat16),
+        in_specs=[smem, vmem, vmem, vmem, vmem],
+        out_specs=vmem,
+        scratch_shapes=[pltpu.VMEM((tokens, patch), jnp.float32)],
+    )(
+        jnp.stack([own, cfg_index.astype(jnp.int32)]),
+        received,
+        weight,
+        noise,
+        jnp.asarray(pick, jnp.bfloat16),
+    )
+    got = lax.all_to_all(
+        shares.reshape(groups * cfg_count, tile, 2 * patch),
+        ("blk", "seq", "cfg"),
+        split_axis=0,
+        concat_axis=0,
+        tiled=True,
+    )
+    place = jnp.stack(
+        [blk_index, seq_index, cfg_index, jnp.int32(grid_cols), jnp.int32(seq_count * high)]
+    ).astype(jnp.int32)
+    frames_out = frames // cfg_count
+    return pl.pallas_call(
+        conv_kernel,
+        out_shape=jax.ShapeDtypeStruct((frames_out, 2 * high, 2 * wide, channels), jnp.bfloat16),
+        in_specs=[smem] + [vmem] * 7,
+        out_specs=vmem,
+        scratch_shapes=[pltpu.VMEM((4, 48 * ZCH, channels), jnp.bfloat16)],
+    )(
+        place,
+        got,
+        jnp.tile(latent_std, 2 * patch // ZCH)[None, :],
+        jnp.tile(latent_mean, 2 * patch // ZCH)[None, :],
+        jnp.asarray(window_rows(frames_out, high, wide)),
+        conv_weight.reshape(27, ZCH, channels),
+        conv_bias[None, :],
+        jnp.asarray(output_order(frames_out, high, wide), jnp.bfloat16),
+    )
+
+
+def chosen(*arrays):
+    groups = lax.axis_size("seq") * lax.axis_size("blk")
+    heads = arrays[0].shape[2] // HDIM
+    if heads % groups == 0:
+        return by_heads(*arrays)
+    return local(*arrays)
+
+
 def solution(mesh):
     in_specs = (
         P("cfg", ("prompt", "blk", "seq"), None),
@@ -208,4 +489,4 @@
         P(),
     )
     out_specs = P(("prompt", "cfg"), "seq", "blk", None)
-    return jax.shard_map(local, mesh=mesh, in_specs=in_specs, out_specs=out_specs, check_vma=False)
+    return jax.shard_map(chosen, mesh=mesh, in_specs=in_specs, out_specs=out_specs, check_vma=False)

time: 95.3 us -> 46.9 us (0.49)
  starting transfers between devices: 39.4 us -> 11.2 us
  waiting for transfers between devices: 38.4 us -> 20.4 us
  Pallas kernels: 0 us -> 8.09 us
  local copies, waits for them, and re-layouts: 9.88 us -> 6.25 us
  matrix products: 2.88 us -> 0 us
  other arithmetic: 3.41 us -> 0.56 us
    ppermute x11 -> x0, starting transfers between devices: 20.8 us -> none  [the longest x7 11.7 us: partner(): lax.ppermute(array, axis, [(i, i ^ 1 << apart) for i in range(lax.axis_si...]
    ppermute x11 -> x0, waiting for transfers between devices: 19.2 us -> none  [the longest x7 13.8 us: partner(): lax.ppermute(array, axis, [(i, i ^ 1 << apart) for i in range(lax.axis_si...]
    pallas_call x0 -> x3, Pallas kernels: none -> 8.09 us  [the longest x1 3.2 us: by_heads(): pl.pallas_call(attend_kernel, out_shape=jax.ShapeDtypeStruct((groups, cfg...]
    all_to_all x5 -> x2, starting transfers between devices: 18.6 us -> 11.2 us  [the longest x1 7.28 us: exchange(): lax.all_to_all(packed, ('blk', 'seq'), split_axis=0, concat_axis=0, tiled...]
    all_to_all x10 -> x0, local copies, waits for them, and re-layouts: 4 us -> none  [the longest x2 1.86 us: local(): lax.all_to_all(own_query, 'seq', split_axis=1, concat_axis=0, tiled=True)]
    dot_general x11 -> x0, matrix products: 2.88 us -> none  [the longest x4 1.29 us: one_block(): jnp.einsum('hqk,khd->qhd', weights, value_block, preferred_element_type=j...]
    another operation x2 -> x5, local copies, waits for them, and re-layouts: 0.01 us -> 1.94 us  [the longest x1 0.66 us: by_heads(): jnp.stack([blk_index, seq_index, cfg_index, jnp.int32(grid_cols), jnp.int...]
    unnamed x5 -> x0, other arithmetic: 1.88 us -> none
  transfers between devices with their start and end apart: 16 -> 2, of which waited for: 11 -> 2; matrix products, arithmetic and copies ran while one was open for 4% -> 8% of each run, Pallas kernels for 0% -> 0%
where the time goes in v1:
time: 46.9 us; the launch traced here: 46.5 us
  waiting for transfers between devices  20.4 us (43%)
  starting transfers between devices  11.2 us (24%)
  Pallas kernels  8.09 us (17%)
  local copies, waits for them, and re-layouts  6.25 us (13%)
  other arithmetic  0.56 us (1%)
    all_to_all x1, waiting for transfers between devices, exchange(): lax.all_to_all(packed, ('blk', 'seq'), split_axis=0, concat_axis=0, tiled...  14.5 us
    all_to_all x1, starting transfers between devices, exchange(): lax.all_to_all(packed, ('blk', 'seq'), split_axis=0, concat_axis=0, tiled...  7.28 us
    all_to_all x1, waiting for transfers between devices, by_heads(): lax.all_to_all(shares.reshape(groups * cfg_count, tile, 2 * patch), ('blk...  5.83 us
    all_to_all x1, starting transfers between devices, by_heads(): lax.all_to_all(shares.reshape(groups * cfg_count, tile, 2 * patch), ('blk...  3.88 us
    pallas_call x1, Pallas kernels, by_heads(): pl.pallas_call(attend_kernel, out_shape=jax.ShapeDtypeStruct((groups, cfg...  3.2 us
    pallas_call x1, Pallas kernels, by_heads(): pl.pallas_call(conv_kernel, out_shape=jax.ShapeDtypeStruct((frames_out, 2...  2.65 us
    unnamed x13, local copies, waits for them, and re-layouts  2.3 us
    pallas_call x1, Pallas kernels, by_heads(): pl.pallas_call(pack_kernel, out_shape=(jax.ShapeDtypeStruct((groups, bloc...  2.23 us
  transfers between devices with their start and end apart: 2, of which 2 were waited for; matrix products, arithmetic and copies ran while one was open for 8% of the time, Pallas kernels for 0%

profile of v1, /device:TPU:0, one launch (start us, length us, event | category | flops | bytes accessed | tf_op | source)
XLA Modules:
  0.0 46.5 jit_solution(591390895048135383)
XLA Ops:
  0.0 0.0 copy-start
  0.0 2.2 %shard_map.127 = (bf16[8,24,1536]{2,1,0:T(8,128)(2,1)}, f32[24,64]{1,0:T(8,128)}) custom-call(s32[1,24]{1,0:T(1,128)} %bitcast.18, s32[1]{0:T(128)} %bitcast.5.start_ref, bf16[24,4096]{1,0:T(8,128)(2,1)} %bitcast.15, bf16[24,4096]{1,0:T(8,128)(2,1)} %bitcast.16, bf16[24,4096]{1,0:T(8,128)(2,1)} %bitcast.17, f32[24,64]{1,0:T(8,128)} %noisy_ref.1), custom_call_target="tpu_custom_call" | custom-call | tf_op jit(solution)/shard_map/pallas_call | solution.py:405
  2.2 7.3 %all-to-all-start = ((bf16[8,24,1536]{2,1,0:T(8,128)(2,1)}), bf16[8,24,1536]{2,1,0:T(8,128)(2,1)S(1)}, u32[]{:S(2)}, u32[]{:S(2)}) async-start(bf16[8,24,1536]{2,1,0:T(8,128)(2,1)} %get-tuple-element.7), calls=%async_computation | async-start | bytes 1179648 | tf_op jit(solution)/shard_map/all_to_all | solution.py:371
  9.5 0.0 copy-done
  9.5 0.8 %copy.16.weight_ref = bf16[512,64]{1,0:T(8,128)(2,1)} copy(bf16[512,64]{0,1:T(8,128)(2,1)S(1)} %constant_dynamic-slice_fusion) | data formatting | bytes 131072
  10.3 0.6 %pad_add_fusion.place_ref = s32[2]{0:T(128)} fusion(s32[1]{0:T(128)} %bitcast.2, s32[1]{0:T(128)} %bitcast.3), kind=kLoop, calls=%fused_computation | loop fusion | flops 2 | bytes 16 | tf_op jit(solution)/shard_map/stack | solution.py:435
  10.9 14.5 %all-to-all-done = bf16[8,24,1536]{2,1,0:T(8,128)(2,1)S(1)} async-done(((bf16[8,24,1536]{2,1,0:T(8,128)(2,1)}), bf16[8,24,1536]{2,1,0:T(8,128)(2,1)S(1)}, u32[]{:S(2)}, u32[]{:S(2)}) %all-to-all-start) | async-done | bytes 589856 | tf_op jit(solution)/shard_map/all_to_all | solution.py:371
  25.4 0.0 copy-start.1
  25.4 0.8 %copy-done.1 = bf16[8,24,1536]{2,1,0:T(8,128)(2,1)} copy-done((bf16[8,24,1536]{2,1,0:T(8,128)(2,1)}, bf16[8,24,1536]{2,1,0:T(8,128)(2,1)S(1)}, u32[]{:S(2)}) %copy-start.1) | copy-done | bytes 589848
  26.2 3.2 %shard_map.128 = bf16[8,2,40,128]{3,2,1,0:T(8,128)(2,1)} custom-call(s32[2]{0:T(128)} %pad_add_fusion.place_ref, bf16[192,1536]{1,0:T(8,128)(2,1)} %bitcast.12, bf16[512,64]{1,0:T(8,128)(2,1)} %copy.16.weight_ref, f32[24,64]{1,0:T(8,128)} %get-tuple-element.8.noise_ref, bf16[320,96]{1,0:T(8,128)(2,1)} %constant.31.clone.pick_ref), custom_call_target="tpu_custom_call" | custom-call | tf_op jit(solution)/shard_map/pallas_call | solution.py:428
  29.4 0.0 copy-start.4
  29.4 3.9 %all-to-all-start.1 = ((bf16[16,40,128]{2,1,0:T(8,128)(2,1)}), bf16[16,40,128]{2,1,0:T(8,128)(2,1)S(1)}, u32[]{:S(2)}, u32[]{:S(2)}) async-start(bf16[16,40,128]{2,1,0:T(8,128)(2,1)} %bitcast.13), calls=%async_computation.1 | async-start | bytes 327680 | tf_op jit(solution)/shard_map/all_to_all | solution.py:441
  33.3 0.0 copy-done.4
  33.3 0.0 copy-start.5
  33.3 0.7 %broadcast_in_dim_tile.6.std_ref = f32[1,128]{1,0:T(1,128)} reshape(f32[8,16]{1,0:T(8,128)S(1)} %tile.4) | data formatting | bytes 1024 | tf_op jit(solution)/shard_map/broadcast_in_dim;tile | solution.py:461
  34.0 0.0 copy-done.5
  34.0 0.6 %broadcast_in_dim_tile.7.mean_ref = f32[1,128]{1,0:T(1,128)} reshape(f32[8,16]{1,0:T(8,128)S(1)} %tile.5) | data formatting | bytes 1024 | tf_op jit(solution)/shard_map/broadcast_in_dim;tile | solution.py:462
  34.6 0.1 copy-done.3
  34.7 0.6 %broadcast_in_dim.11.bias_ref = f32[1,384]{1,0:T(1,128)} reshape(f32[384]{0:T(512)S(1)} %copy-done.3) | data formatting | bytes 3072 | tf_op jit(solution)/shard_map/broadcast_in_dim | solution.py:465
  35.2 0.7 %stack.22.place_ref = s32[5]{0:T(128)} concatenate(s32[1]{0:T(128)} %bitcast, s32[1]{0:T(128)} %bitcast.1, s32[1]{0:T(128)} %bitcast.2, s32[1]{0:T(128)} %constant.8.clone.1, s32[1]{0:T(128)} %constant.9.clone.1), dimensions={0} | concatenate | bytes 40 | tf_op jit(solution)/shard_map/stack | solution.py:448
  35.9 5.8 %all-to-all-done.1.got_ref = bf16[16,40,128]{2,1,0:T(8,128)(2,1)S(1)} async-done(((bf16[16,40,128]{2,1,0:T(8,128)(2,1)}), bf16[16,40,128]{2,1,0:T(8,128)(2,1)S(1)}, u32[]{:S(2)}, u32[]{:S(2)}) %all-to-all-start.1) | async-done | bytes 163872 | tf_op jit(solution)/shard_map/all_to_all | solution.py:441
  41.7 0.7 %copy-done.2 = bf16[16,40,128]{2,1,0:T(8,128)(2,1)} copy-done((bf16[16,40,128]{2,1,0:T(8,128)(2,1)}, bf16[16,40,128]{2,1,0:T(8,128)(2,1)S(1)}, u32[]{:S(2)}) %copy-start.2) | copy-done | bytes 163864
  42.4 2.7 %shard_map.129 = bf16[2,4,6,384]{3,2,1,0:T(8,128)(2,1)} custom-call(s32[5]{0:T(128)} %stack.22.place_ref, bf16[16,40,128]{2,1,0:T(8,128)(2,1)} %copy-done.2, f32[1,128]{1,0:T(1,128)} %broadcast_in_dim_tile.6.std_ref, f32[1,128]{1,0:T(1,128)} %broadcast_in_dim_tile.7.mean_ref, s32[288,1]{1,0:T(8,128)} %constant.32.clone.mesh_ref, ...), custom_call_target="tpu_custom_call" | custom-call | tf_op jit(solution)/shard_map/pallas_call | solution.py:452
  45.1 1.4 %copy.15 = bf16[2,4,6,384]{3,1,2,0:T(4,128)(2,1)} copy(bf16[2,4,6,384]{3,2,1,0:T(8,128)(2,1)} %shard_map.129) | data formatting | bytes 73728 | tf_op jit(solution)/shard_map/pallas_call | solution.py:452
  (5 shorter events, 0.0 us)
Async XLA Ops:
  0.0 9.5 %copy-start = (bf16[4096,64]{0,1:T(8,128)(2,1)S(1)}, bf16[4096,64]{0,1:T(8,128)(2,1)}, u32[]{:S(2)}) copy-start(bf16[4096,64]{0,1:T(8,128)(2,1)} %param.18) | copy-start | bytes 1572868
  2.2 23.2 %all-to-all-start = ((bf16[8,24,1536]{2,1,0:T(8,128)(2,1)}), bf16[8,24,1536]{2,1,0:T(8,128)(2,1)S(1)}, u32[]{:S(2)}, u32[]{:S(2)}) async-start(bf16[8,24,1536]{2,1,0:T(8,128)(2,1)} %get-tuple-element.7), calls=%async_computation | async-start | bytes 1179648 | tf_op jit(solution)/shard_map/all_to_all | solution.py:371
  25.4 0.8 %copy-start.1 = (bf16[8,24,1536]{2,1,0:T(8,128)(2,1)}, bf16[8,24,1536]{2,1,0:T(8,128)(2,1)S(1)}, u32[]{:S(2)}) copy-start(bf16[8,24,1536]{2,1,0:T(8,128)(2,1)S(1)} %all-to-all-done) | copy-start | bytes 1769476
  29.4 3.9 %copy-start.4 = (f32[16]{0:T(128)S(1)}, f32[16]{0:T(128)}, u32[]{:S(2)}) copy-start(f32[16]{0:T(128)} %param.19) | copy-start | bytes 196
  29.4 12.3 %all-to-all-start.1 = ((bf16[16,40,128]{2,1,0:T(8,128)(2,1)}), bf16[16,40,128]{2,1,0:T(8,128)(2,1)S(1)}, u32[]{:S(2)}, u32[]{:S(2)}) async-start(bf16[16,40,128]{2,1,0:T(8,128)(2,1)} %bitcast.13), calls=%async_computation.1 | async-start | bytes 327680 | tf_op jit(solution)/shard_map/all_to_all | solution.py:441
  33.3 0.7 %copy-start.5 = (f32[16]{0:T(128)S(1)}, f32[16]{0:T(128)}, u32[]{:S(2)}) copy-start(f32[16]{0:T(128)} %param.20) | copy-start | bytes 196
  34.0 0.7 %copy-start.3 = (f32[384]{0:T(512)S(1)}, f32[384]{0:T(512)}, u32[]{:S(2)}) copy-start(f32[384]{0:T(512)} %param.22) | copy-start | bytes 4612
  41.7 0.7 %copy-start.2 = (bf16[16,40,128]{2,1,0:T(8,128)(2,1)}, bf16[16,40,128]{2,1,0:T(8,128)(2,1)S(1)}, u32[]{:S(2)}) copy-start(bf16[16,40,128]{2,1,0:T(8,128)(2,1)S(1)} %all-to-all-done.1.got_ref) | copy-start | bytes 491524

commit v2 on v1

--- a/solution.py
+++ b/solution.py
@@ -197,9 +197,10 @@
     return output.reshape(half, tile_rows, tile_cols, conv_weight.shape[4]).astype(jnp.bfloat16)
 
 
-def pack_kernel(order_ref, start_ref, q_ref, k_ref, v_ref, noisy_ref, send_ref, noise_ref):
+def pack_kernel(order_ref, start_ref, q_ref, k_ref, v_ref, head_ref, noisy_ref, send_ref, noise_ref):
     groups, rows, width = send_ref.shape
-    feat = width // 3
+    patch = noise_ref.shape[1]
+    feat = width * HDIM // (2 * HDIM + patch)
     slot = order_ref[...] - start_ref[0]
     hit = lax.broadcasted_iota(jnp.int32, (rows, rows), 0) == slot
     selector = hit.astype(jnp.bfloat16)
@@ -209,7 +210,21 @@
         cols = slice(group * feat, (group + 1) * feat)
         send_ref[group, :, :feat] = ordered[:, cols]
         send_ref[group, :, feat : 2 * feat] = k_ref[:, cols]
-        send_ref[group, :, 2 * feat :] = v_ref[:, cols]
+        for head in range(0, feat // HDIM, 2):
+            low = group * feat + head * HDIM
+            both = [
+                lax.dot_general(
+                    v_ref[:, at : at + HDIM],
+                    head_ref[:, at : at + HDIM],
+                    (((1,), (1,)), ((), ())),
+                    preferred_element_type=jnp.float32,
+                )
+                for at in (low, low + HDIM)
+            ]
+            at = 2 * feat + head * patch
+            send_ref[group, :, at : at + 2 * patch] = jnp.concatenate(both, axis=1).astype(
+                jnp.bfloat16
+            )
     noise_ref[...] = jnp.dot(
         hit.astype(jnp.float32),
         noisy_ref[...],
@@ -218,17 +233,20 @@
     )
 
 
-def attend_kernel(place_ref, qkv_ref, weight_ref, noise_ref, pick_ref, out_ref, acc_ref):
+def attend_kernel(place_ref, qkv_ref, noise_ref, pick_ref, out_ref, acc_ref):
     tokens, width = qkv_ref.shape
-    feat = width // 3
+    patch = acc_ref.shape[1]
+    feat = width * HDIM // (2 * HDIM + patch)
     block = noise_ref.shape[0]
     scale = 1.0 / math.sqrt(HDIM)
-    total_velocity = jnp.zeros(acc_ref.shape, jnp.float32)
+    wide_velocity = jnp.zeros((tokens, 2 * patch), jnp.float32)
+    lane = lax.broadcasted_iota(jnp.int32, (tokens, 2 * patch), 1)
     for head in range(feat // HDIM):
         low = head * HDIM
         query = qkv_ref[:, low : low + HDIM]
         key = qkv_ref[:, feat + low : feat + low + HDIM]
-        value = qkv_ref[:, 2 * feat + low : 2 * feat + low + HDIM]
+        pair = 2 * feat + head // 2 * 2 * patch
+        value = qkv_ref[:, pair : pair + 2 * patch]
         scores = (
             lax.dot_general(
                 query, key, (((1,), (1,)), ((), ())), preferred_element_type=jnp.float32
@@ -240,13 +258,11 @@
         mixed = jnp.dot(
             expo.astype(jnp.bfloat16), value, preferred_element_type=jnp.float32
         )
-        mixed = (mixed / total).astype(jnp.bfloat16)
-        total_velocity = total_velocity + jnp.dot(
-            mixed, weight_ref[low : low + HDIM, :], preferred_element_type=jnp.float32
-        )
+        mine = lane // patch == head % 2
+        wide_velocity = wide_velocity + jnp.where(mine, mixed / total, 0.0)
     is_cond = place_ref[1] == 0
     factor = jnp.where(is_cond, -NOISE_LEVEL * GUIDE, -NOISE_LEVEL * (1.0 - GUIDE))
-    acc_ref[...] = total_velocity * factor
+    acc_ref[...] = (wide_velocity[:, :patch] + wide_velocity[:, patch:]) * factor
     rows = pl.ds(pl.multiple_of(place_ref[0] * block, 8), block)
     acc_ref[rows, :] = acc_ref[rows, :] + noise_ref[...] * jnp.where(is_cond, 1.0, 0.0)
     share = acc_ref[...].astype(jnp.bfloat16)
@@ -261,38 +277,22 @@
 
 
 def conv_kernel(
-    place_ref, got_ref, std_ref, mean_ref, mesh_ref, weight_ref, bias_ref, order_ref, out_ref, big_ref
+    place_ref,
+    got_ref,
+    std_ref,
+    mean_ref,
+    mesh_ref,
+    weight_ref,
+    bias_ref,
+    order_ref,
+    out_ref,
+    big_ref,
 ):
-    frames_out, tile_rows, tile_cols, channels = out_ref.shape
+    big_ref[...] = jnp.zeros(big_ref.shape, big_ref.dtype)
+    frames_out, tile_cols, tile_rows, channels = out_ref.shape
     wide = tile_cols // 2
     high = tile_rows // 2
     shares, rows, lanes = got_ref.shape
-    summed = got_ref[0].astype(jnp.float32)
-    for share in range(1, shares):
-        summed = summed + got_ref[share].astype(jnp.float32)
-    span = wide + 2
-    tall = high + 2
-    row = lax.broadcasted_iota(jnp.int32, (rows, lanes), 0)
-    col_at = place_ref[0] * wide - 1 + row % span
-    row_at = place_ref[1] * high - 1 + row // span % tall
-    inside = (
-        (col_at >= 0) & (col_at < place_ref[3]) & (row_at >= 0) & (row_at < place_ref[4])
-    )
-    pixels = jnp.where(inside, summed * std_ref[...] + mean_ref[...], 0.0)
-    half = lanes // 2
-    flat = jnp.concatenate([pixels[:, :half], pixels[:, half:]], axis=0)
-    count = 2 * rows
-    moved = pltpu.roll(flat, count - 1, 0)
-    pairs = jnp.concatenate([flat, moved], axis=1).astype(jnp.bfloat16)
-    wanted = mesh_ref[:, 0:1] + place_ref[2] * (frames_out * tall * span)
-    hits = (lax.broadcasted_iota(jnp.int32, (mesh_ref.shape[0], count), 1) == wanted).astype(
-        jnp.bfloat16
-    )
-    pieces = jnp.dot(hits, pairs, preferred_element_type=jnp.float32).astype(jnp.bfloat16)
-    part = frames_out * high * wide
-    part = (part + 15) // 16 * 16
-    big_ref[...] = jnp.zeros(big_ref.shape, big_ref.dtype)
-    results = []
     for down in range(2):
         for right in range(2):
             which = down * 2 + right
@@ -305,6 +305,34 @@
                         big_ref[which, at * ZCH : (at + 1) * ZCH, :] = weight_ref[
                             (step_t * 3 + step_y) * 3 + step_x
                         ]
+    summed = got_ref[0].astype(jnp.float32)
+    for share in range(1, shares):
+        summed = summed + got_ref[share].astype(jnp.float32)
+    span = wide + 2
+    tall = high + 2
+    row = lax.broadcasted_iota(jnp.int32, (rows, lanes), 0)
+    col_at = place_ref[0] * wide - 1 + row % span
+    row_at = place_ref[1] * high - 1 + row // span % tall
+    inside = (
+        (col_at >= 0) & (col_at < place_ref[3]) & (row_at >= 0) & (row_at < place_ref[4])
+    )
+    pixels = jnp.where(inside, summed * std_ref[...] + mean_ref[...], 0.0)
+    half = lanes // 2
+    flat = jnp.concatenate([pixels[:, :half], pixels[:, half:]], axis=0)
+    count = 2 * rows
+    moved = pltpu.roll(flat, count - 1, 0)
+    pairs = jnp.concatenate([flat, moved], axis=1).astype(jnp.bfloat16)
+    wanted = mesh_ref[:, 0:1] + place_ref[2] * (frames_out * tall * span)
+    hits = (lax.broadcasted_iota(jnp.int32, (mesh_ref.shape[0], count), 1) == wanted).astype(
+        jnp.bfloat16
+    )
+    pieces = jnp.dot(hits, pairs, preferred_element_type=jnp.float32).astype(jnp.bfloat16)
+    part = frames_out * high * wide
+    part = (part + 15) // 16 * 16
+    results = []
+    for down in range(2):
+        for right in range(2):
+            which = down * 2 + right
             columns = []
             for step_t in range(3):
                 for near in range(2):
@@ -317,9 +345,9 @@
     final = jnp.dot(order_ref[...], together, preferred_element_type=jnp.float32)
     final = final.astype(jnp.bfloat16)
     for frame in range(frames_out):
-        for y in range(tile_rows):
-            at = (frame * tile_rows + y) * 8
-            out_ref[frame, y] = final[at : at + tile_cols]
+        for x in range(tile_cols):
+            at = (frame * tile_cols + x) * 8
+            out_ref[frame, x] = final[at : at + tile_rows]
 
 
 def tile_rows_of(seq_count, blk_count, frames, high, wide):
@@ -357,13 +385,13 @@
 
 def output_order(frames_out, high, wide):
     part = (frames_out * high * wide + 15) // 16 * 16
-    table = np.zeros((frames_out * 2 * high * 8, 4 * part), np.float32)
+    table = np.zeros((frames_out * 2 * wide * 8, 4 * part), np.float32)
     for frame in range(frames_out):
         for y in range(2 * high):
             for x in range(2 * wide):
                 which = (y % 2) * 2 + x % 2
                 source = which * part + (frame * high + y // 2) * wide + x // 2
-                table[(frame * 2 * high + y) * 8 + x, source] = 1.0
+                table[(frame * 2 * wide + x) * 8 + y, source] = 1.0
     return table
 
 
@@ -394,6 +422,7 @@
     tokens = groups * block
     feat = queries.shape[2] // groups
     patch = noisy_latents.shape[1]
+    width = 2 * feat + feat // HDIM * patch
     channels = conv_weight.shape[4]
     own = (blk_index * seq_count + seq_index).astype(jnp.int32)
     frames = blk_count
@@ -405,10 +434,10 @@
     packed, noise = pl.pallas_call(
         pack_kernel,
         out_shape=(
-            jax.ShapeDtypeStruct((groups, block, 3 * feat), jnp.bfloat16),
-            jax.ShapeDtypeStruct((block, patch), jnp.float32),
+            pltpu.VMEM((groups, block, width), jnp.bfloat16),
+            pltpu.VMEM((block, patch), jnp.float32),
         ),
-        in_specs=[vmem, smem, vmem, vmem, vmem, vmem],
+        in_specs=[vmem, smem, vmem, vmem, vmem, vmem, vmem],
         out_specs=(vmem, vmem),
     )(
         patch_order[None, :],
@@ -416,10 +445,12 @@
         queries[0],
         key_states[0],
         value_states[0],
+        head_weight.T,
         noisy_latents,
     )
-    received = exchange(packed).reshape(tokens, 3 * feat)
-    weight = lax.dynamic_slice_in_dim(head_weight, own * feat, feat, 0)
+    received = pltpu.with_memory_space_constraint(
+        exchange(packed).reshape(tokens, width), pltpu.VMEM
+    )
     pick = (
         np.arange(tokens // 2)[None, :]
         == tile_rows_of(seq_count, blk_count, frames, high, wide)[:, None]
@@ -427,15 +458,16 @@
     tile = frames // 2 * (high + 2) * (wide + 2)
     shares = pl.pallas_call(
         attend_kernel,
-        out_shape=jax.ShapeDtypeStruct((groups, cfg_count, tile, 2 * patch), jnp.bfloat16),
-        in_specs=[smem, vmem, vmem, vmem, vmem],
+        out_shape=pltpu.VMEM((groups, cfg_count, tile, 2 * patch), jnp.bfloat16),
+        in_specs=[smem] + [vmem] * 3,
         out_specs=vmem,
-        scratch_shapes=[pltpu.VMEM((tokens, patch), jnp.float32)],
+        scratch_shapes=[
+            pltpu.VMEM((tokens, patch), jnp.float32),
+        ],
     )(
         jnp.stack([own, cfg_index.astype(jnp.int32)]),
         received,
-        weight,
-        noise,
+        pltpu.with_memory_space_constraint(noise, pltpu.VMEM),
         jnp.asarray(pick, jnp.bfloat16),
     )
     got = lax.all_to_all(
@@ -449,15 +481,17 @@
         [blk_index, seq_index, cfg_index, jnp.int32(grid_cols), jnp.int32(seq_count * high)]
     ).astype(jnp.int32)
     frames_out = frames // cfg_count
-    return pl.pallas_call(
+    features = pl.pallas_call(
         conv_kernel,
-        out_shape=jax.ShapeDtypeStruct((frames_out, 2 * high, 2 * wide, channels), jnp.bfloat16),
+        out_shape=jax.ShapeDtypeStruct((frames_out, 2 * wide, 2 * high, channels), jnp.bfloat16),
         in_specs=[smem] + [vmem] * 7,
         out_specs=vmem,
-        scratch_shapes=[pltpu.VMEM((4, 48 * ZCH, channels), jnp.bfloat16)],
+        scratch_shapes=[
+            pltpu.VMEM((4, 48 * ZCH, channels), jnp.bfloat16),
+        ],
     )(
         place,
-        got,
+        pltpu.with_memory_space_constraint(got, pltpu.VMEM),
         jnp.tile(latent_std, 2 * patch // ZCH)[None, :],
         jnp.tile(latent_mean, 2 * patch // ZCH)[None, :],
         jnp.asarray(window_rows(frames_out, high, wide)),
@@ -465,12 +499,13 @@
         conv_bias[None, :],
         jnp.asarray(output_order(frames_out, high, wide), jnp.bfloat16),
     )
+    return features.transpose(0, 2, 1, 3)
 
 
 def chosen(*arrays):
     groups = lax.axis_size("seq") * lax.axis_size("blk")
     heads = arrays[0].shape[2] // HDIM
-    if heads % groups == 0:
+    if heads % (2 * groups) == 0:
         return by_heads(*arrays)
     return local(*arrays)
 

time: 46.9 us -> 41.7 us (0.89)
  local copies, waits for them, and re-layouts: 6.25 us -> 2.63 us
  waiting for transfers between devices: 20.4 us -> 18.9 us
    unnamed x13 -> x6, local copies, waits for them, and re-layouts: 2.3 us -> 0.1 us
    pallas_call x1 -> x0, local copies, waits for them, and re-layouts: 1.43 us -> none  [by_heads(): pl.pallas_call(conv_kernel, out_shape=jax.ShapeDtypeStruct((frames_out, 2...]
    all_to_all x1, waiting for transfers between devices: 14.5 us -> 13.1 us  [exchange(): lax.all_to_all(packed, ('blk', 'seq'), split_axis=0, concat_axis=0, tiled...]
where the time goes in v2:
time: 41.7 us; the launch traced here: 41.3 us
  waiting for transfers between devices  18.9 us (45%)
  starting transfers between devices  11.2 us (27%)
  Pallas kernels  7.88 us (19%)
  local copies, waits for them, and re-layouts  2.63 us (6%)
  other arithmetic  0.64 us (2%)
    all_to_all x1, waiting for transfers between devices, exchange(): lax.all_to_all(packed, ('blk', 'seq'), split_axis=0, concat_axis=0, tiled...  13.1 us
    all_to_all x1, starting transfers between devices, exchange(): lax.all_to_all(packed, ('blk', 'seq'), split_axis=0, concat_axis=0, tiled...  7.28 us
    all_to_all x1, waiting for transfers between devices, by_heads(): lax.all_to_all(shares.reshape(groups * cfg_count, tile, 2 * patch), ('blk...  5.77 us
    all_to_all x1, starting transfers between devices, by_heads(): lax.all_to_all(shares.reshape(groups * cfg_count, tile, 2 * patch), ('blk...  3.88 us
    pallas_call x1, Pallas kernels, by_heads(): pl.pallas_call(pack_kernel, out_shape=(pltpu.VMEM((groups, block, width),...  2.7 us
    pallas_call x1, Pallas kernels, by_heads(): pl.pallas_call(attend_kernel, out_shape=pltpu.VMEM((groups, cfg_count, ti...  2.65 us
    pallas_call x1, Pallas kernels, by_heads(): pl.pallas_call(conv_kernel, out_shape=jax.ShapeDtypeStruct((frames_out, 2...  2.54 us
  transfers between devices with their start and end apart: 2, of which 2 were waited for; matrix products, arithmetic and copies ran while one was open for 8% of the time, Pallas kernels for 0%

profile of v2, /device:TPU:0, one launch (start us, length us, event | category | flops | bytes accessed | tf_op | source)
XLA Modules:
  0.0 41.3 jit_solution(3117658641720561429)
XLA Ops:
  0.0 2.7 %shard_map.127 = (bf16[8,24,1280]{2,1,0:T(8,128)(2,1)}, f32[24,64]{1,0:T(8,128)S(1)}) custom-call(s32[1,24]{1,0:T(1,128)} %bitcast.20, s32[1]{0:T(128)} %bitcast.5.start_ref, bf16[24,4096]{1,0:T(8,128)(2,1)} %bitcast.17, bf16[24,4096]{1,0:T(8,128)(2,1)} %bitcast.18, bf16[24,4096]{1,0:T(8,128)(2,1)} %bitcast.19, bf16[64,4096]{1,0:T(8,128)(2,1)} %bitcast.15, ...), custom_call_target="tpu_custom_call" | custom-call | tf_op jit(solution)/shard_map/pallas_call | solution.py:434
  2.7 7.3 %all-to-all-start = ((bf16[8,24,1280]{2,1,0:T(8,128)(2,1)}), bf16[8,24,1280]{2,1,0:T(8,128)(2,1)S(1)}, u32[]{:S(2)}, u32[]{:S(2)}) async-start(bf16[8,24,1280]{2,1,0:T(8,128)(2,1)} %get-tuple-element.7), calls=%async_computation | async-start | bytes 983040 | tf_op jit(solution)/shard_map/all_to_all | solution.py:399
  10.0 0.6 %pad_add_fusion.place_ref = s32[2]{0:T(128)} fusion(s32[1]{0:T(128)} %bitcast.2, s32[1]{0:T(128)} %bitcast.3), kind=kLoop, calls=%fused_computation | loop fusion | flops 2 | bytes 16 | tf_op jit(solution)/shard_map/stack | solution.py:468
  10.6 13.1 %all-to-all-done = bf16[8,24,1280]{2,1,0:T(8,128)(2,1)S(1)} async-done(((bf16[8,24,1280]{2,1,0:T(8,128)(2,1)}), bf16[8,24,1280]{2,1,0:T(8,128)(2,1)S(1)}, u32[]{:S(2)}, u32[]{:S(2)}) %all-to-all-start) | async-done | bytes 491552 | tf_op jit(solution)/shard_map/all_to_all | solution.py:399
  23.8 2.6 %shard_map.128 = bf16[8,2,40,128]{3,2,1,0:T(8,128)(2,1)} custom-call(s32[2]{0:T(128)} %pad_add_fusion.place_ref, bf16[192,1280]{1,0:T(8,128)(2,1)S(1)} %bitcast.14, f32[24,64]{1,0:T(8,128)S(1)} %get-tuple-element.8.noise_ref, bf16[320,96]{1,0:T(8,128)(2,1)} %constant.25.clone.pick_ref), custom_call_target="tpu_custom_call" | custom-call | tf_op jit(solution)/shard_map/pallas_call | solution.py:459
  26.4 0.0 copy-start.1
  26.4 3.9 %all-to-all-start.1 = ((bf16[16,40,128]{2,1,0:T(8,128)(2,1)}), bf16[16,40,128]{2,1,0:T(8,128)(2,1)S(1)}, u32[]{:S(2)}, u32[]{:S(2)}) async-start(bf16[16,40,128]{2,1,0:T(8,128)(2,1)} %bitcast.11), calls=%async_computation.1 | async-start | bytes 327680 | tf_op jit(solution)/shard_map/all_to_all | solution.py:473
  30.3 0.0 copy-done.1
  30.3 0.0 copy-start.2
  30.3 0.7 %broadcast_in_dim_tile.6.std_ref = f32[1,128]{1,0:T(1,128)} reshape(f32[8,16]{1,0:T(8,128)S(1)} %tile.4) | data formatting | bytes 1024 | tf_op jit(solution)/shard_map/broadcast_in_dim;tile | solution.py:495
  31.0 0.0 copy-done.2
  31.0 0.0 copy-start
  31.0 0.6 %broadcast_in_dim_tile.7.mean_ref = f32[1,128]{1,0:T(1,128)} reshape(f32[8,16]{1,0:T(8,128)S(1)} %tile.5) | data formatting | bytes 1024 | tf_op jit(solution)/shard_map/broadcast_in_dim;tile | solution.py:496
  31.6 0.1 copy-done
  31.7 0.6 %broadcast_in_dim.11.bias_ref = f32[1,384]{1,0:T(1,128)} reshape(f32[384]{0:T(512)S(1)} %copy-done) | data formatting | bytes 3072 | tf_op jit(solution)/shard_map/broadcast_in_dim | solution.py:499
  32.3 0.7 %stack.22.place_ref = s32[5]{0:T(128)} concatenate(s32[1]{0:T(128)} %bitcast, s32[1]{0:T(128)} %bitcast.1, s32[1]{0:T(128)} %bitcast.2, s32[1]{0:T(128)} %constant.8.clone.1, s32[1]{0:T(128)} %constant.22.clone.1), dimensions={0} | concatenate | bytes 40 | tf_op jit(solution)/shard_map/stack | solution.py:480
  33.0 5.8 %all-to-all-done.1.got_ref = bf16[16,40,128]{2,1,0:T(8,128)(2,1)S(1)} async-done(((bf16[16,40,128]{2,1,0:T(8,128)(2,1)}), bf16[16,40,128]{2,1,0:T(8,128)(2,1)S(1)}, u32[]{:S(2)}, u32[]{:S(2)}) %all-to-all-start.1) | async-done | bytes 163872 | tf_op jit(solution)/shard_map/all_to_all | solution.py:473
  38.7 2.5 %shard_map.129 = bf16[2,6,4,384]{3,2,1,0:T(4,128)(2,1)} custom-call(s32[5]{0:T(128)} %stack.22.place_ref, bf16[16,40,128]{2,1,0:T(8,128)(2,1)S(1)} %all-to-all-done.1.got_ref, f32[1,128]{1,0:T(1,128)} %broadcast_in_dim_tile.6.std_ref, f32[1,128]{1,0:T(1,128)} %broadcast_in_dim_tile.7.mean_ref, s32[288,1]{1,0:T(8,128)} %constant.26.clone.mesh_ref, ...), custom_call_target="tpu_custom_call" | custom-call | tf_op jit(solution)/shard_map/pallas_call | solution.py:484
  (2 shorter events, 0.0 us)
Async XLA Ops:
  2.7 21.1 %all-to-all-start = ((bf16[8,24,1280]{2,1,0:T(8,128)(2,1)}), bf16[8,24,1280]{2,1,0:T(8,128)(2,1)S(1)}, u32[]{:S(2)}, u32[]{:S(2)}) async-start(bf16[8,24,1280]{2,1,0:T(8,128)(2,1)} %get-tuple-element.7), calls=%async_computation | async-start | bytes 983040 | tf_op jit(solution)/shard_map/all_to_all | solution.py:399
  26.4 3.9 %copy-start.1 = (f32[16]{0:T(128)S(1)}, f32[16]{0:T(128)}, u32[]{:S(2)}) copy-start(f32[16]{0:T(128)} %param.19) | copy-start | bytes 196
  26.4 12.3 %all-to-all-start.1 = ((bf16[16,40,128]{2,1,0:T(8,128)(2,1)}), bf16[16,40,128]{2,1,0:T(8,128)(2,1)S(1)}, u32[]{:S(2)}, u32[]{:S(2)}) async-start(bf16[16,40,128]{2,1,0:T(8,128)(2,1)} %bitcast.11), calls=%async_computation.1 | async-start | bytes 327680 | tf_op jit(solution)/shard_map/all_to_all | solution.py:473
  30.3 0.7 %copy-start.2 = (f32[16]{0:T(128)S(1)}, f32[16]{0:T(128)}, u32[]{:S(2)}) copy-start(f32[16]{0:T(128)} %param.20) | copy-start | bytes 196
  31.0 0.7 %copy-start = (f32[384]{0:T(512)S(1)}, f32[384]{0:T(512)}, u32[]{:S(2)}) copy-start(f32[384]{0:T(512)} %param.22) | copy-start | bytes 4612
